TPU v7x, 32 devices: a whole 2x2x4 slice. The times are simulated.
32 devices in a mesh: tp: 4 (over z), cp: 8 (over y, x, core).
Axes of the slice: x: 2, y: 2, z: 4, core: 2. Of those that a mesh axis runs over, the one named last changes fastest.
Arguments:
- q_raw: bfloat16 [4096, 16, 128], P('cp', 'tp'), parts along dimension 1
- k_raw: bfloat16 [4096, 8, 128], P('cp', 'tp'), parts along dimension 1
- v_raw: bfloat16 [4096, 8, 128], P('cp', 'tp'), parts along dimension 1
- positions: int32 [4096], P('cp')
- seq_ids: int32 [4096], P('cp')
- q_gain: bfloat16 [128], replicated
- k_gain: bfloat16 [128], replicated
Outputs:
- output 1: bfloat16 [4096, 16, 128], P('cp', 'tp'), parts along dimension 1
- output 2: float32 [4096, 16], P('cp', 'tp'), parts along dimension 1
There are 4 independent parts. A program takes and returns all parts, laid end to end along the dimension named above; an argument that names none is the same for every part.
All inputs are finite; a program needn't handle non-finite values.
Results may differ from a plain program's by a relative error of at most 0.017719.
Values are sent between devices in bfloat16 or wider.
A program may use at most 1 GiB of HBM per device.

v0:
```python
import functools
import math

import jax
import jax.numpy as jnp
import numpy as np
from jax import lax
from jax.experimental import pallas as pl
from jax.experimental.pallas import tpu as pltpu
from jax.sharding import PartitionSpec as P

THETA = 1000000.0
EPS = 1e-6
NEG_BIG = -1e30
D = 128
HALF = 256
ROWS = 512
C_EXP = (D ** -0.5) * math.log2(math.e)
SCALE = D ** -0.5
F32 = jnp.float32
BF16 = jnp.bfloat16


def nt(a, b):
    return lax.dot_general(a, b, (((1,), (1,)), ((), ())), preferred_element_type=F32)


def nn(a, b):
    return lax.dot_general(a, b, (((1,), (0,)), ((), ())), preferred_element_type=F32)


def kernel(q_hbm, k_hbm, v_hbm, pos_hbm, seq_hbm, qg_hbm, kg_hbm, freq_hbm, out_ref, lse_out,
           q_in, k_in, v_in, pos_v, seq_v, qg_v, kg_v, freq_v, f_scr, cs_scr, perm, perm_t,
           kbuf, vbuf, kst, vst, qbuf, qst, kaug, m_scr, l_scr, acc, ost, obuf, lst, lbuf, pbuf,
           in_sem, s_kx, s_vx, s_p, s_q, s_fk, s_fv, s_o, s_l, r_k, r_v, r_q, r_o, r_l):
    me = lax.axis_index("cp")
    core = lax.rem(me, 2)
    chip = lax.div(me, 2)
    x = lax.rem(chip, 2)
    y = lax.div(chip, 2)
    xchip = chip + 1 - 2 * x
    ychip = chip + 2 - 4 * y
    other = 1 - core
    partner = 2 * chip + other

    def rcopy(src, dst, ssem, rsem, dev):
        return pltpu.make_async_remote_copy(src_ref=src, dst_ref=dst, send_sem=ssem, recv_sem=rsem,
                                            device_id={"cp": dev}, device_id_type=pl.DeviceIdType.MESH)

    barrier = pltpu.get_barrier_semaphore()
    peers = [partner, 2 * xchip, 2 * xchip + 1, 2 * ychip, 2 * ychip + 1]
    for peer in peers:
        pl.semaphore_signal(barrier, inc=1, device_id={"cp": peer}, device_id_type=pl.DeviceIdType.MESH)

    ins = [(v_hbm, v_in), (seq_hbm, seq_v), (pos_hbm, pos_v), (k_hbm, k_in), (kg_hbm, kg_v), (freq_hbm, freq_v),
           (q_hbm, q_in), (qg_hbm, qg_v)]
    in_copies = [pltpu.make_async_copy(src, dst, in_sem.at[n]) for n, (src, dst) in enumerate(ins)]
    for cp in in_copies:
        cp.start()

    in_copies[1].wait()
    seq = seq_v[...]
    row_id = lax.broadcasted_iota(jnp.int32, (8, ROWS), 1).astype(F32)
    sub_id = lax.broadcasted_iota(jnp.int32, (8, ROWS), 0)
    is_seq = jnp.broadcast_to(seq, (8, ROWS)) == sub_id
    seq_f = jnp.where(is_seq, 1.0, 0.0)
    cnt = jnp.sum(seq_f, axis=1, keepdims=True)
    start = jnp.min(jnp.where(is_seq, row_id, float(ROWS)), axis=1, keepdims=True)
    start_row = jnp.sum(seq_f * start, axis=0, keepdims=True)
    cnt_row = jnp.sum(seq_f * cnt, axis=0, keepdims=True)
    off = row_id[:1] - start_row
    late = off * 2.0 >= cnt_row
    dest = start_row * 0.5 + off + jnp.where(late, HALF - 0.5 * cnt_row, 0.0)
    dest_i = dest.astype(jnp.int32)
    for blk in range(4):
        rows = lax.broadcasted_iota(jnp.int32, (128, ROWS), 0) + blk * 128
        perm[pl.ds(blk * 128, 128), :] = jnp.where(rows == dest_i, 1.0, 0.0).astype(BF16)

    in_copies[0].wait()
    f_scr[pl.ds(0, 1024), :] = v_in[...].astype(F32)
    for h in range(2):
        vt = f_scr[pl.ds(h, ROWS, stride=2), :].T.astype(BF16)
        vc = nt(vt, perm[...]).astype(BF16)
        for half in range(2):
            vst[h, half] = vc[:, half * HALF:(half + 1) * HALF]
    for half in range(2):
        vbuf[0, half, core] = vst[core, half]
    pl.semaphore_wait(barrier, 5)

    sends = []

    def send_v(half):
        for h in range(2):
            for t, tchip in enumerate((xchip, ychip)):
                sends.append(rcopy(vst.at[h, half], vbuf.at[1 + t, half, core], s_vx.at[t, h, half],
                                   r_v.at[1 + t, core, half], 2 * tchip + h))
                sends[-1].start()

    def send_k(half):
        for h in range(2):
            for t, tchip in enumerate((xchip, ychip)):
                sends.append(rcopy(kst.at[h, half], kbuf.at[1 + t, half, core], s_kx.at[t, h, half],
                                   r_k.at[1 + t, core, half], 2 * tchip + h))
                sends[-1].start()

    send_v(0)
    for half in range(2):
        sends.append(rcopy(vst.at[other, half], vbuf.at[0, half, core], s_p.at[0, half], r_v.at[0, core, half], partner))
        sends[-1].start()

    in_copies[2].wait()
    in_copies[5].wait()
    angle = freq_v[...] * pos_v[...].astype(F32)
    cs_scr[0] = jnp.cos(angle)
    cs_scr[1] = jnp.sin(angle)

    def norm_rope(rows_f32, gain_v):
        xt = rows_f32.T
        inv = lax.rsqrt(jnp.mean(xt * xt, axis=0, keepdims=True) + EPS)
        gain = jnp.broadcast_to(gain_v[...].astype(F32), (128, D)).T
        gain = jnp.concatenate([gain] * 4, axis=1)
        n = (xt * inv * gain).astype(BF16).astype(F32)
        a, b = n[:64], n[64:]
        cos, sin = cs_scr[0], cs_scr[1]
        return jnp.concatenate([a * cos - b * sin, b * cos + a * sin], axis=0).astype(BF16)

    in_copies[3].wait()
    in_copies[4].wait()
    f_scr[pl.ds(0, 1024), :] = k_in[...].astype(F32)
    for h in range(2):
        kr = norm_rope(f_scr[pl.ds(h, ROWS, stride=2), :], kg_v)
        kc = nt(perm[...], kr).astype(BF16)
        for half in range(2):
            kst[h, half] = kc[half * HALF:(half + 1) * HALF, :]
    for half in range(2):
        kbuf[0, half, core] = kst[core, half]

    send_k(0)
    send_v(1)
    send_k(1)
    for half in range(2):
        sends.append(rcopy(kst.at[other, half], kbuf.at[0, half, core], s_p.at[1, half], r_k.at[0, core, half], partner))
        sends[-1].start()

    in_copies[6].wait()
    in_copies[7].wait()
    f_scr[...] = q_in[...].astype(F32)

    def q_head(h, store):
        qr = norm_rope(f_scr[pl.ds(h, ROWS, stride=4), :], qg_v)
        qc = nt(qr, perm[...]).astype(BF16)
        for half in range(2):
            store(half, qc[:, half * HALF:(half + 1) * HALF])

    for g in range(2):
        def store_other(half, val, g=g):
            qst[half, :, g * HALF:(g + 1) * HALF] = val
        q_head(2 * other + g, store_other)
    for half in range(2):
        sends.append(rcopy(qst.at[half], qbuf.at[half, 0, pl.ds(0, D), :], s_q.at[half], r_q.at[half], partner))
        sends[-1].start()
    for g in range(2):
        def store_own(half, val, g=g):
            qbuf[half, 1, pl.ds(0, D), g * HALF:(g + 1) * HALF] = val
        q_head(2 * core + g, store_own)

    lane_d = lax.broadcasted_iota(jnp.int32, (8, HALF), 1).astype(F32)
    in_run = (lane_d >= start * 0.5) & (lane_d < (start + cnt) * 0.5)
    one_hot = jnp.where(in_run, 1.0, 0.0)
    blocked = jnp.where(in_run, 0.0, NEG_BIG)
    blocked = jnp.where(lax.broadcasted_iota(jnp.int32, (8, HALF), 0) < 4, blocked, 0.0)
    pad = jnp.zeros((D - 8, HALF), F32)
    q_extra = jnp.concatenate([blocked, pad], axis=0).astype(BF16)
    for half in range(2):
        for dev in range(2):
            for g in range(2):
                qbuf[half, dev, pl.ds(D, D), g * HALF:(g + 1) * HALF] = q_extra
    kaug[...] = jnp.concatenate([one_hot, pad], axis=0).T.astype(BF16)

    dest_cols = jnp.broadcast_to(dest, (128, ROWS)).T.astype(jnp.int32)
    for blk in range(4):
        lanes = lax.broadcasted_iota(jnp.int32, (ROWS, 128), 1) + blk * 128
        perm_t[blk // 2, :, (blk % 2) * 128:(blk % 2 + 1) * 128] = jnp.where(lanes == dest_cols, 1.0, 0.0).astype(BF16)

    m_scr[...] = jnp.full(m_scr.shape, NEG_BIG, F32)
    l_scr[...] = jnp.zeros(l_scr.shape, F32)
    acc[...] = jnp.zeros(acc.shape, F32)

    def tile_parts(slot, khalf, qhalf, causal):
        keys = kbuf[slot, khalf].reshape(2 * HALF, D)
        ka = kaug[...]
        keys = jnp.concatenate([keys, jnp.concatenate([ka, ka], axis=0)], axis=1)
        v0 = vbuf[slot, khalf, 0]
        v1 = vbuf[slot, khalf, 1]
        chunks = [(dev, g) for dev in range(2) for g in range(2)]

        def scores(n):
            dev, g = chunks[n]
            s = nn(keys, qbuf[qhalf, dev, :, pl.ds(g * HALF, HALF)])
            if causal:
                abs_dev = core if dev == 1 else other
                krow = lax.broadcasted_iota(jnp.int32, (2 * HALF, HALF), 0)
                qcol = lax.broadcasted_iota(jnp.int32, (2 * HALF, HALF), 1)
                kord = krow + qhalf * jnp.where(krow < HALF, HALF, -HALF)
                qord = qcol + (abs_dev + qhalf * (1 - 2 * abs_dev)) * HALF
                s = jnp.where(kord <= qord, s, NEG_BIG)
            return s

        def soft(n, s):
            dev, g = chunks[n]
            cols = pl.ds(g * HALF, HALF)
            m_old = m_scr[qhalf, dev, :, cols]
            m_new = jnp.maximum(m_old, jnp.max(s, axis=0, keepdims=True))
            p = jnp.exp2((s - m_new) * C_EXP)
            alpha = jnp.exp2((m_old - m_new) * C_EXP)
            m_scr[qhalf, dev, :, cols] = m_new
            l_scr[qhalf, dev, :, cols] = l_scr[qhalf, dev, :, cols] * alpha + jnp.sum(p, axis=0, keepdims=True)
            return p.astype(BF16), alpha

        def out(n, pb, alpha):
            dev, g = chunks[n]
            cols = pl.ds(g * HALF, HALF)
            o = nn(v0, pb[:HALF]) + nn(v1, pb[HALF:])
            acc[qhalf, dev, :, cols] = acc[qhalf, dev, :, cols] * alpha + o

        return scores, soft, out

    def tile(slot, khalf, qhalf, causal):
        scores, soft, out = tile_parts(slot, khalf, qhalf, causal)
        s = scores(0)
        prev = None
        for n in range(4):
            nxt = scores(n + 1) if n < 3 else None
            pb, alpha = soft(n, s)
            if prev is not None:
                out(n - 1, *prev)
            prev = (pb, alpha)
            s = nxt
        out(3, *prev)

    def got_k(slot, dev, half):
        rcopy(kst.at[0, half], kbuf.at[slot, half, dev], s_kx.at[0, 0, half], r_k.at[slot, dev, half], partner).wait_recv()

    def got_v(slot, dev, half):
        rcopy(vst.at[0, half], vbuf.at[slot, half, dev], s_vx.at[0, 0, half], r_v.at[slot, dev, half], partner).wait_recv()

    for half in range(2):
        got_v(0, other, half)
        got_k(0, other, half)
        rcopy(qst.at[half], qbuf.at[half, 0, pl.ds(0, D), :], s_q.at[half], r_q.at[half], partner).wait_recv()

    def own_body(half, carry):
        tile(0, half, half, True)
        return carry

    lax.fori_loop(0, 2, own_body, 0)

    def fwd_v(dev, half):
        slot, to = (2, xchip) if dev == 0 else (1, ychip)
        return rcopy(vbuf.at[slot, half, dev], vbuf.at[3, half, dev], s_fv.at[dev, half], r_v.at[3, dev, half], 2 * to + core)

    def fwd_k(dev, half):
        slot, to = (2, xchip) if dev == 0 else (1, ychip)
        return rcopy(kbuf.at[slot, half, dev], kbuf.at[3, half, dev], s_fk.at[dev, half], r_k.at[3, dev, half], 2 * to + core)

    def body(idx, carry):
        @pl.when(idx == 1)
        def _():
            for dev in range(2):
                got_v(2 - dev, dev, 0)
                fwd_v(dev, 0).start()
            for dev in range(2):
                got_k(2 - dev, dev, 0)
                fwd_k(dev, 0).start()
            got_v(1, 0, 0)
            got_k(1, 0, 0)

        @pl.when(idx == 2)
        def _():
            got_v(2, 1, 0)
            got_k(2, 1, 0)

        @pl.when(idx == 3)
        def _():
            for dev in range(2):
                got_k(2 - dev, dev, 1)
                fwd_k(dev, 1).start()
            for dev in range(2):
                got_v(2 - dev, dev, 1)
                fwd_v(dev, 1).start()
            got_v(1, 0, 1)
            got_k(1, 0, 1)

        @pl.when(idx == 4)
        def _():
            got_v(2, 1, 1)
            got_k(2, 1, 1)

        @pl.when(idx == 5)
        def _():
            for dev in range(2):
                got_v(3, dev, 0)
                got_k(3, dev, 0)

        second = (idx // 3) * (1 - idx // 5)
        slot = idx - 2 * second - 2 * (idx // 5)
        late_needed = (1 - y) + (idx % 2) * (y - x)
        sel = second * late_needed
        tile(slot, sel, 1 - second + sel, False)
        return carry

    lax.fori_loop(0, 6, body, 0)

    done = y
    last = 1 - y

    def place(grp, half, first):
        for g in range(2):
            rows = pl.ds(2 * grp + g, ROWS, stride=4)
            val = nt(perm_t[half], obuf[grp, half, g])
            f_scr[rows, :] = val if first else f_scr[rows, :] + val

    def give(half, n):
        return rcopy(ost.at[half], obuf.at[core, half], s_o.at[n], r_o.at[n], partner)

    def take(half, n):
        rcopy(ost.at[half], obuf.at[other, half], s_o.at[n], r_o.at[n], partner).wait_recv()

    for g in range(2):
        cols = pl.ds(g * HALF, HALF)
        ost[done, g] = (acc[done, 0, :, cols] * (1.0 / l_scr[done, 0, :, cols])).astype(BF16)
    give(done, 0).start()
    for g in range(2):
        cols = pl.ds(g * HALF, HALF)
        obuf[core, done, g] = (acc[done, 1, :, cols] * (1.0 / l_scr[done, 1, :, cols])).astype(BF16)
    place(core, done, True)

    for dev in range(2):
        got_k(3, dev, 1)
    scores, soft, _ = tile_parts(3, last, last, False)
    s = scores(0)
    for n in range(4):
        nxt = scores(n + 1) if n < 3 else None
        pb, alpha = soft(n, s)
        pbuf[n] = pb
        cols = pl.ds((n % 2) * HALF, HALF)
        acc[last, n // 2, :, cols] = acc[last, n // 2, :, cols] * alpha
        s = nxt
    for dev in range(2):
        for half in range(2):
            for g in range(2):
                cols = pl.ds(g * HALF, HALF)
                val = m_scr[half, dev, :, cols] * SCALE + jnp.log(l_scr[half, dev, :, cols])
                if dev == 0:
                    lst[pl.ds(g, 1), half * HALF:(half + 1) * HALF] = val
                else:
                    lbuf[core, pl.ds(g, 1), half * HALF:(half + 1) * HALF] = val
        if dev == 0:
            l_send = rcopy(lst, lbuf.at[core], s_l.at[0], r_l.at[0], partner)
            l_send.start()
    take(done, 0)
    place(other, done, True)

    for dev in range(2):
        got_v(3, dev, 1)
    for n in range(4):
        cols = pl.ds((n % 2) * HALF, HALF)
        dev, g = n // 2, n % 2
        o = nn(vbuf[3, last, 0], pbuf[n, :HALF, :]) + nn(vbuf[3, last, 1], pbuf[n, HALF:, :])
        o = ((acc[last, dev, :, cols] + o) * (1.0 / l_scr[last, dev, :, cols])).astype(BF16)
        if dev == 0:
            ost[last, g] = o
        else:
            obuf[core, last, g] = o
        if n == 1:
            give(last, 1).start()
    place(core, last, False)
    rcopy(lst, lbuf.at[other], s_l.at[0], r_l.at[0], partner).wait_recv()
    lse = jnp.concatenate([lbuf[0, :2], lbuf[1, :2]], axis=0)
    hi = lse.astype(BF16).astype(F32)
    rest = lse - hi
    mid = rest.astype(BF16).astype(F32)
    pieces = jnp.concatenate([hi, mid, rest - mid, jnp.zeros((4, ROWS), F32)], axis=0).astype(BF16)
    pieces = nn(pieces, perm[...])
    lse_out[...] = pieces[0:4] + pieces[4:8] + pieces[8:12]
    take(last, 1)
    place(other, last, False)
    out_ref[...] = f_scr[...].astype(BF16)

    for cp in sends:
        cp.wait_send()
    for half in range(2):
        for dev in range(2):
            fwd_v(dev, half).wait_send()
            fwd_k(dev, half).wait_send()
    give(done, 0).wait_send()
    give(last, 1).wait_send()
    l_send.wait_send()


def write_out(o_ref, l_ref, o_hbm, l_hbm, sem):
    copies = [pltpu.make_async_copy(o_ref, o_hbm, sem.at[0]), pltpu.make_async_copy(l_ref, l_hbm, sem.at[1])]
    for cp in copies:
        cp.start()
    for cp in copies:
        cp.wait()


def solution(mesh):
    freq = (THETA ** (-(np.arange(64, dtype=np.float64) * 2.0) / D)).astype(np.float32)
    freq = np.broadcast_to(freq[:, None], (64, ROWS)).copy()
    any_spec = pl.BlockSpec(memory_space=pl.ANY)
    dma = pltpu.SemaphoreType.DMA
    vm = pltpu.VMEM

    def per_device(q_raw, k_raw, v_raw, positions, seq_ids, q_gain, k_gain):
        call = pl.pallas_call(
            kernel,
            out_shape=(jax.ShapeDtypeStruct((4 * ROWS, D), BF16), jax.ShapeDtypeStruct((4, ROWS), F32)),
            in_specs=[any_spec] * 8,
            out_specs=(pl.BlockSpec(memory_space=pltpu.VMEM), pl.BlockSpec(memory_space=pltpu.VMEM)),
            scratch_shapes=[
                vm((4 * ROWS, D), BF16), vm((2 * ROWS, D), BF16), vm((2 * ROWS, D), BF16),
                vm((1, ROWS), jnp.int32), vm((1, ROWS), jnp.int32), vm((1, D), BF16), vm((1, D), BF16),
                vm((64, ROWS), F32),
                vm((4 * ROWS, D), F32), vm((2, 64, ROWS), F32), vm((ROWS, ROWS), BF16), vm((2, ROWS, HALF), BF16),
                vm((4, 2, 2, HALF, D), BF16), vm((4, 2, 2, D, HALF), BF16),
                vm((2, 2, HALF, D), BF16), vm((2, 2, D, HALF), BF16),
                vm((2, 2, 2 * D, 2 * HALF), BF16), vm((2, D, 2 * HALF), BF16), vm((HALF, D), BF16),
                vm((2, 2, 1, 2 * HALF), F32), vm((2, 2, 1, 2 * HALF), F32), vm((2, 2, D, 2 * HALF), F32),
                vm((2, 2, D, HALF), BF16), vm((2, 2, 2, D, HALF), BF16), vm((8, ROWS), F32), vm((2, 8, ROWS), F32),
                vm((4, 2 * HALF, HALF), BF16),
                dma((8,)), dma((2, 2, 2)), dma((2, 2, 2)), dma((2, 2)), dma((2,)), dma((2, 2)), dma((2, 2)),
                dma((2,)), dma((1,)), dma((4, 2, 2)), dma((4, 2, 2)), dma((2,)), dma((2,)), dma((1,)),
            ],
            compiler_params=pltpu.CompilerParams(collective_id=0, has_side_effects=True, vmem_limit_bytes=40000 * 1024),
        )
        args = (q_raw.reshape(4 * ROWS, D), k_raw.reshape(2 * ROWS, D), v_raw.reshape(2 * ROWS, D),
                positions.reshape(1, ROWS), seq_ids.reshape(1, ROWS), q_gain.reshape(1, D), k_gain.reshape(1, D),
                jnp.asarray(freq))
        args = [pltpu.with_memory_space_constraint(a, pltpu.HBM) for a in args]
        out, lse = call(*args)
        out, lse = pl.pallas_call(
            write_out,
            out_shape=(jax.ShapeDtypeStruct((4 * ROWS, D), BF16), jax.ShapeDtypeStruct((4, ROWS), F32)),
            in_specs=[pl.BlockSpec(memory_space=pltpu.VMEM)] * 2,
            out_specs=(pl.BlockSpec(memory_space=pltpu.HBM), pl.BlockSpec(memory_space=pltpu.HBM)),
            scratch_shapes=[dma((2,))],
            compiler_params=pltpu.CompilerParams(vmem_limit_bytes=1024*1024),
        )(out, lse)
        return out.reshape(ROWS, 4, D), lse.T

    return jax.shard_map(per_device, mesh=mesh, in_specs=(P("cp", "tp", None), P("cp", "tp", None), P("cp", "tp", None), P("cp"), P("cp"), P(), P()), out_specs=(P("cp", "tp", None), P("cp", "tp")), check_vma=False)
```

profile of v0, /device:TPU:0, one launch (start us, length us, event | category | flops | bytes accessed | tf_op | source)
XLA Modules:
  0.0 26.7 jit_solution(8977981881454196403)
XLA Ops:
  0.6 25.2 %shard_map.95 = (bf16[2048,128]{1,0:T(8,128)(2,1)S(1)}, f32[4,512]{1,0:T(4,128)S(1)}) custom-call(bf16[2048,128]{1,0:T(8,128)(2,1)} %bitcast.9, bf16[1024,128]{1,0:T(8,128)(2,1)} %bitcast.10, bf16[1024,128]{1,0:T(8,128)(2,1)} %bitcast.11, s32[1,512]{1,0:T(1,128)} %bitcast.12, s32[1,512]{1,0:T(1,128)} %bitcast.13, bf16[1,128]{1,0:T(2,128)(2,1)} %bitcast.14, ...), custom_call_target="tpu_custom_call" | custom-call | tf_op jit(solution)/shard_map/pallas_call | solution.py:442
  25.8 0.8 %shard_map.96 = (bf16[2048,128]{1,0:T(8,128)(2,1)}, f32[4,512]{1,0:T(4,128)}) custom-call(bf16[2048,128]{1,0:T(8,128)(2,1)S(1)} %get-tuple-element.6.o_ref, f32[4,512]{1,0:T(4,128)S(1)} %get-tuple-element.7.l_ref), custom_call_target="tpu_custom_call" | custom-call | tf_op jit(solution)/shard_map/pallas_call | solution.py:443
where the time goes:
time: 26.8 us; the launch traced here: 26.7 us
  Pallas kernels  26 us (97%)
  between operations  0.64 us (2%)
    pallas_call x1, Pallas kernels, per_device(): out, lse = call(*args)  25.2 us
    pallas_call x1, Pallas kernels, per_device(): pl.pallas_call(write_out, out_shape=(jax.ShapeDtypeStruct((4 * ROWS, D),...  0.81 us

commit v1 on v0

--- a/solution.py
+++ b/solution.py
@@ -31,8 +31,8 @@
 
 def kernel(q_hbm, k_hbm, v_hbm, pos_hbm, seq_hbm, qg_hbm, kg_hbm, freq_hbm, out_ref, lse_out,
            q_in, k_in, v_in, pos_v, seq_v, qg_v, kg_v, freq_v, f_scr, cs_scr, perm, perm_t,
-           kbuf, vbuf, kst, vst, qbuf, qst, kaug, m_scr, l_scr, acc, ost, obuf, lst, lbuf, pbuf,
-           in_sem, s_kx, s_vx, s_p, s_q, s_fk, s_fv, s_o, s_l, r_k, r_v, r_q, r_o, r_l):
+           kbuf, vbuf, vraw, kst, vst, qbuf, qst, kaug, m_scr, l_scr, acc, ost, obuf, lst, lbuf, pbuf,
+           in_sem, ready, s_raw, r_raw, s_kx, s_v, s_p, s_q, s_fk, s_fv, s_o, s_l, r_k, r_v, r_q, r_o, r_l):
     me = lax.axis_index("cp")
     core = lax.rem(me, 2)
     chip = lax.div(me, 2)
@@ -48,15 +48,25 @@
                                             device_id={"cp": dev}, device_id_type=pl.DeviceIdType.MESH)
 
     barrier = pltpu.get_barrier_semaphore()
-    peers = [partner, 2 * xchip, 2 * xchip + 1, 2 * ychip, 2 * ychip + 1]
-    for peer in peers:
+    for peer in (2 * xchip, 2 * ychip + 1, partner):
         pl.semaphore_signal(barrier, inc=1, device_id={"cp": peer}, device_id_type=pl.DeviceIdType.MESH)
 
     ins = [(v_hbm, v_in), (seq_hbm, seq_v), (pos_hbm, pos_v), (k_hbm, k_in), (kg_hbm, kg_v), (freq_hbm, freq_v),
            (q_hbm, q_in), (qg_hbm, qg_v)]
     in_copies = [pltpu.make_async_copy(src, dst, in_sem.at[n]) for n, (src, dst) in enumerate(ins)]
-    for cp in in_copies:
-        cp.start()
+    for n in (1, 2, 5, 3, 4, 0, 6, 7):
+        in_copies[n].start()
+
+    pl.semaphore_wait(barrier, 3)
+    pl.semaphore_signal(ready, inc=1, device_id={"cp": partner}, device_id_type=pl.DeviceIdType.MESH)
+
+    def raw_v(t):
+        tchip = xchip + t * (ychip - xchip)
+        return rcopy(v_hbm, vraw.at[t], s_raw.at[t], r_raw.at[t], 2 * tchip + core)
+
+    raw_v(core).start()
+    pl.semaphore_wait(ready, 1)
+    raw_v(other).start()
 
     in_copies[1].wait()
     seq = seq_v[...]
@@ -76,25 +86,7 @@
         rows = lax.broadcasted_iota(jnp.int32, (128, ROWS), 0) + blk * 128
         perm[pl.ds(blk * 128, 128), :] = jnp.where(rows == dest_i, 1.0, 0.0).astype(BF16)
 
-    in_copies[0].wait()
-    f_scr[pl.ds(0, 1024), :] = v_in[...].astype(F32)
-    for h in range(2):
-        vt = f_scr[pl.ds(h, ROWS, stride=2), :].T.astype(BF16)
-        vc = nt(vt, perm[...]).astype(BF16)
-        for half in range(2):
-            vst[h, half] = vc[:, half * HALF:(half + 1) * HALF]
-    for half in range(2):
-        vbuf[0, half, core] = vst[core, half]
-    pl.semaphore_wait(barrier, 5)
-
     sends = []
-
-    def send_v(half):
-        for h in range(2):
-            for t, tchip in enumerate((xchip, ychip)):
-                sends.append(rcopy(vst.at[h, half], vbuf.at[1 + t, half, core], s_vx.at[t, h, half],
-                                   r_v.at[1 + t, core, half], 2 * tchip + h))
-                sends[-1].start()
 
     def send_k(half):
         for h in range(2):
@@ -103,10 +95,23 @@
                                    r_k.at[1 + t, core, half], 2 * tchip + h))
                 sends[-1].start()
 
-    send_v(0)
-    for half in range(2):
-        sends.append(rcopy(vst.at[other, half], vbuf.at[0, half, core], s_p.at[0, half], r_v.at[0, core, half], partner))
-        sends[-1].start()
+    def v_share(slot, half):
+        return rcopy(vst.at[slot, half], vbuf.at[slot, half, core], s_v.at[slot, half], r_v.at[slot, core, half], partner)
+
+    def split_v(src, slot):
+        f_scr[pl.ds(0, 2 * ROWS), :] = src[...].astype(F32)
+        for mine in range(2):
+            h = core if mine else other
+            vt = f_scr[pl.ds(h, ROWS, stride=2), :].T.astype(BF16)
+            vc = nt(vt, perm[...]).astype(BF16)
+            for half in range(2):
+                part = vc[:, half * HALF:(half + 1) * HALF]
+                if mine:
+                    vbuf[slot, half, core] = part
+                else:
+                    vst[slot, half] = part
+        for half in range(2):
+            v_share(slot, half).start()
 
     in_copies[2].wait()
     in_copies[5].wait()
@@ -136,11 +141,13 @@
         kbuf[0, half, core] = kst[core, half]
 
     send_k(0)
-    send_v(1)
     send_k(1)
     for half in range(2):
-        sends.append(rcopy(kst.at[other, half], kbuf.at[0, half, core], s_p.at[1, half], r_k.at[0, core, half], partner))
+        sends.append(rcopy(kst.at[other, half], kbuf.at[0, half, core], s_p.at[half], r_k.at[0, core, half], partner))
         sends[-1].start()
+
+    in_copies[0].wait()
+    split_v(v_in, 0)
 
     in_copies[6].wait()
     in_copies[7].wait()
@@ -242,7 +249,7 @@
         rcopy(kst.at[0, half], kbuf.at[slot, half, dev], s_kx.at[0, 0, half], r_k.at[slot, dev, half], partner).wait_recv()
 
     def got_v(slot, dev, half):
-        rcopy(vst.at[0, half], vbuf.at[slot, half, dev], s_vx.at[0, 0, half], r_v.at[slot, dev, half], partner).wait_recv()
+        rcopy(vst.at[0, half], vbuf.at[slot, half, dev], s_v.at[0, half], r_v.at[slot, dev, half], partner).wait_recv()
 
     for half in range(2):
         got_v(0, other, half)
@@ -266,18 +273,21 @@
     def body(idx, carry):
         @pl.when(idx == 1)
         def _():
+            for t in range(2):
+                raw_v(t).wait_recv()
+                split_v(vraw.at[t], 1 + t)
+            for half in range(2):
+                for t in range(2):
+                    got_v(1 + t, other, half)
             for dev in range(2):
-                got_v(2 - dev, dev, 0)
                 fwd_v(dev, 0).start()
             for dev in range(2):
                 got_k(2 - dev, dev, 0)
                 fwd_k(dev, 0).start()
-            got_v(1, 0, 0)
             got_k(1, 0, 0)
 
         @pl.when(idx == 2)
         def _():
-            got_v(2, 1, 0)
             got_k(2, 1, 0)
 
         @pl.when(idx == 3)
@@ -286,14 +296,11 @@
                 got_k(2 - dev, dev, 1)
                 fwd_k(dev, 1).start()
             for dev in range(2):
-                got_v(2 - dev, dev, 1)
                 fwd_v(dev, 1).start()
-            got_v(1, 0, 1)
             got_k(1, 0, 1)
 
         @pl.when(idx == 4)
         def _():
-            got_v(2, 1, 1)
             got_k(2, 1, 1)
 
         @pl.when(idx == 5)
@@ -389,6 +396,11 @@
 
     for cp in sends:
         cp.wait_send()
+    for t in range(2):
+        raw_v(t).wait_send()
+    for slot in range(3):
+        for half in range(2):
+            v_share(slot, half).wait_send()
     for half in range(2):
         for dev in range(2):
             fwd_v(dev, half).wait_send()
@@ -425,12 +437,12 @@
                 vm((64, ROWS), F32),
                 vm((4 * ROWS, D), F32), vm((2, 64, ROWS), F32), vm((ROWS, ROWS), BF16), vm((2, ROWS, HALF), BF16),
                 vm((4, 2, 2, HALF, D), BF16), vm((4, 2, 2, D, HALF), BF16),
-                vm((2, 2, HALF, D), BF16), vm((2, 2, D, HALF), BF16),
+                vm((2, 2 * ROWS, D), BF16), vm((2, 2, HALF, D), BF16), vm((3, 2, D, HALF), BF16),
                 vm((2, 2, 2 * D, 2 * HALF), BF16), vm((2, D, 2 * HALF), BF16), vm((HALF, D), BF16),
                 vm((2, 2, 1, 2 * HALF), F32), vm((2, 2, 1, 2 * HALF), F32), vm((2, 2, D, 2 * HALF), F32),
                 vm((2, 2, D, HALF), BF16), vm((2, 2, 2, D, HALF), BF16), vm((8, ROWS), F32), vm((2, 8, ROWS), F32),
                 vm((4, 2 * HALF, HALF), BF16),
-                dma((8,)), dma((2, 2, 2)), dma((2, 2, 2)), dma((2, 2)), dma((2,)), dma((2, 2)), dma((2, 2)),
+                dma((8,)), pltpu.SemaphoreType.REGULAR, dma((2,)), dma((2,)), dma((2, 2, 2)), dma((3, 2)), dma((2,)), dma((2,)), dma((2, 2)), dma((2, 2)),
                 dma((2,)), dma((1,)), dma((4, 2, 2)), dma((4, 2, 2)), dma((2,)), dma((2,)), dma((1,)),
             ],
             compiler_params=pltpu.CompilerParams(collective_id=0, has_side_effects=True, vmem_limit_bytes=40000 * 1024),

time: 26.8 us -> 25.5 us (0.951)
  Pallas kernels: 26 us -> 24.7 us
    pallas_call x1, Pallas kernels: 25.2 us -> 23.9 us  [per_device(): out, lse = call(*args)]
where the time goes in v1:
time: 25.5 us; the launch traced here: 25.4 us
  Pallas kernels  24.7 us (97%)
  between operations  0.64 us (3%)
    pallas_call x1, Pallas kernels, per_device(): out, lse = call(*args)  23.9 us
    pallas_call x1, Pallas kernels, per_device(): pl.pallas_call(write_out, out_shape=(jax.ShapeDtypeStruct((4 * ROWS, D),...  0.81 us

profile of v1, /device:TPU:0, one launch (start us, length us, event | category | flops | bytes accessed | tf_op | source)
XLA Modules:
  0.0 25.4 jit_solution(10193704075939814793)
XLA Ops:
  0.6 23.9 %shard_map.95 = (bf16[2048,128]{1,0:T(8,128)(2,1)S(1)}, f32[4,512]{1,0:T(4,128)S(1)}) custom-call(bf16[2048,128]{1,0:T(8,128)(2,1)} %bitcast.9, bf16[1024,128]{1,0:T(8,128)(2,1)} %bitcast.10, bf16[1024,128]{1,0:T(8,128)(2,1)} %bitcast.11, s32[1,512]{1,0:T(1,128)} %bitcast.12, s32[1,512]{1,0:T(1,128)} %bitcast.13, bf16[1,128]{1,0:T(2,128)(2,1)} %bitcast.14, ...), custom_call_target="tpu_custom_call" | custom-call | tf_op jit(solution)/shard_map/pallas_call | solution.py:454
  24.5 0.8 %shard_map.96 = (bf16[2048,128]{1,0:T(8,128)(2,1)}, f32[4,512]{1,0:T(4,128)}) custom-call(bf16[2048,128]{1,0:T(8,128)(2,1)S(1)} %get-tuple-element.6.o_ref, f32[4,512]{1,0:T(4,128)S(1)} %get-tuple-element.7.l_ref), custom_call_target="tpu_custom_call" | custom-call | tf_op jit(solution)/shard_map/pallas_call | solution.py:455

commit v2 on v1

--- a/solution.py
+++ b/solution.py
@@ -32,7 +32,7 @@
 def kernel(q_hbm, k_hbm, v_hbm, pos_hbm, seq_hbm, qg_hbm, kg_hbm, freq_hbm, out_ref, lse_out,
            q_in, k_in, v_in, pos_v, seq_v, qg_v, kg_v, freq_v, f_scr, cs_scr, perm, perm_t,
            kbuf, vbuf, vraw, kst, vst, qbuf, qst, kaug, m_scr, l_scr, acc, ost, obuf, lst, lbuf, pbuf,
-           in_sem, ready, s_raw, r_raw, s_kx, s_v, s_p, s_q, s_fk, s_fv, s_o, s_l, r_k, r_v, r_q, r_o, r_l):
+           in_sem, ready, s_raw, r_raw, r_own, r_share, r_k, r_far, r_o, r_l):
     me = lax.axis_index("cp")
     core = lax.rem(me, 2)
     chip = lax.div(me, 2)
@@ -47,6 +47,17 @@
         return pltpu.make_async_remote_copy(src_ref=src, dst_ref=dst, send_sem=ssem, recv_sem=rsem,
                                             device_id={"cp": dev}, device_id_type=pl.DeviceIdType.MESH)
 
+    s_k, s_own, s_share, s_fwd, s_o, s_l = (in_sem.at[n] for n in (1, 2, 3, 4, 5, 0))
+
+    def sized(kib):
+        return kbuf.at[pl.ds(0, kib // 256)] if kib >= 256 else kbuf.at[0, pl.ds(0, kib // 128)]
+
+    def sent(sem, kib):
+        rcopy(sized(kib), sized(kib), sem, r_l.at[0], partner).wait_send()
+
+    def arrived(sem, kib):
+        rcopy(sized(kib), sized(kib), s_l, sem, partner).wait_recv()
+
     barrier = pltpu.get_barrier_semaphore()
     for peer in (2 * xchip, 2 * ychip + 1, partner):
         pl.semaphore_signal(barrier, inc=1, device_id={"cp": peer}, device_id_type=pl.DeviceIdType.MESH)
@@ -62,7 +73,7 @@
 
     def raw_v(t):
         tchip = xchip + t * (ychip - xchip)
-        return rcopy(v_hbm, vraw.at[t], s_raw.at[t], r_raw.at[t], 2 * tchip + core)
+        return rcopy(v_hbm, vraw.at[t], s_raw.at[0], r_raw.at[t], 2 * tchip + core)
 
     raw_v(core).start()
     pl.semaphore_wait(ready, 1)
@@ -86,17 +97,10 @@
         rows = lax.broadcasted_iota(jnp.int32, (128, ROWS), 0) + blk * 128
         perm[pl.ds(blk * 128, 128), :] = jnp.where(rows == dest_i, 1.0, 0.0).astype(BF16)
 
-    sends = []
-
     def send_k(half):
         for h in range(2):
             for t, tchip in enumerate((xchip, ychip)):
-                sends.append(rcopy(kst.at[h, half], kbuf.at[1 + t, half, core], s_kx.at[t, h, half],
-                                   r_k.at[1 + t, core, half], 2 * tchip + h))
-                sends[-1].start()
-
-    def v_share(slot, half):
-        return rcopy(vst.at[slot, half], vbuf.at[slot, half, core], s_v.at[slot, half], r_v.at[slot, core, half], partner)
+                rcopy(kst.at[h, half], kbuf.at[1 + t, core, half], s_k, r_k.at[t, half], 2 * tchip + h).start()
 
     def split_v(src, slot):
         f_scr[pl.ds(0, 2 * ROWS), :] = src[...].astype(F32)
@@ -107,11 +111,10 @@
             for half in range(2):
                 part = vc[:, half * HALF:(half + 1) * HALF]
                 if mine:
-                    vbuf[slot, half, core] = part
+                    vbuf[slot, core, half] = part
                 else:
                     vst[slot, half] = part
-        for half in range(2):
-            v_share(slot, half).start()
+        rcopy(vst.at[slot], vbuf.at[slot, core], s_share if slot else s_own, r_share.at[0] if slot else r_own.at[0], partner).start()
 
     in_copies[2].wait()
     in_copies[5].wait()
@@ -138,13 +141,11 @@
         for half in range(2):
             kst[h, half] = kc[half * HALF:(half + 1) * HALF, :]
     for half in range(2):
-        kbuf[0, half, core] = kst[core, half]
+        kbuf[0, core, half] = kst[core, half]
 
     send_k(0)
     send_k(1)
-    for half in range(2):
-        sends.append(rcopy(kst.at[other, half], kbuf.at[0, half, core], s_p.at[half], r_k.at[0, core, half], partner))
-        sends[-1].start()
+    rcopy(kst.at[other], kbuf.at[0, core], s_own, r_own.at[0], partner).start()
 
     in_copies[0].wait()
     split_v(v_in, 0)
@@ -163,9 +164,7 @@
         def store_other(half, val, g=g):
             qst[half, :, g * HALF:(g + 1) * HALF] = val
         q_head(2 * other + g, store_other)
-    for half in range(2):
-        sends.append(rcopy(qst.at[half], qbuf.at[half, 0, pl.ds(0, D), :], s_q.at[half], r_q.at[half], partner))
-        sends[-1].start()
+    rcopy(qst, qbuf.at[:, 0, pl.ds(0, D), :], s_own, r_own.at[0], partner).start()
     for g in range(2):
         def store_own(half, val, g=g):
             qbuf[half, 1, pl.ds(0, D), g * HALF:(g + 1) * HALF] = val
@@ -194,11 +193,11 @@
     acc[...] = jnp.zeros(acc.shape, F32)
 
     def tile_parts(slot, khalf, qhalf, causal):
-        keys = kbuf[slot, khalf].reshape(2 * HALF, D)
         ka = kaug[...]
-        keys = jnp.concatenate([keys, jnp.concatenate([ka, ka], axis=0)], axis=1)
-        v0 = vbuf[slot, khalf, 0]
-        v1 = vbuf[slot, khalf, 1]
+        keys = [jnp.concatenate([kbuf[slot, dev, khalf], ka], axis=1) for dev in range(2)]
+        keys = jnp.concatenate(keys, axis=0)
+        v0 = vbuf[slot, 0, khalf]
+        v1 = vbuf[slot, 1, khalf]
         chunks = [(dev, g) for dev in range(2) for g in range(2)]
 
         def scores(n):
@@ -245,16 +244,7 @@
             s = nxt
         out(3, *prev)
 
-    def got_k(slot, dev, half):
-        rcopy(kst.at[0, half], kbuf.at[slot, half, dev], s_kx.at[0, 0, half], r_k.at[slot, dev, half], partner).wait_recv()
-
-    def got_v(slot, dev, half):
-        rcopy(vst.at[0, half], vbuf.at[slot, half, dev], s_v.at[0, half], r_v.at[slot, dev, half], partner).wait_recv()
-
-    for half in range(2):
-        got_v(0, other, half)
-        got_k(0, other, half)
-        rcopy(qst.at[half], qbuf.at[half, 0, pl.ds(0, D), :], s_q.at[half], r_q.at[half], partner).wait_recv()
+    arrived(r_own.at[0], 512)
 
     def own_body(half, carry):
         tile(0, half, half, True)
@@ -264,11 +254,11 @@
 
     def fwd_v(dev, half):
         slot, to = (2, xchip) if dev == 0 else (1, ychip)
-        return rcopy(vbuf.at[slot, half, dev], vbuf.at[3, half, dev], s_fv.at[dev, half], r_v.at[3, dev, half], 2 * to + core)
+        return rcopy(vbuf.at[slot, dev, half], vbuf.at[3, dev, half], s_fwd, r_far.at[2 * half], 2 * to + core)
 
     def fwd_k(dev, half):
         slot, to = (2, xchip) if dev == 0 else (1, ychip)
-        return rcopy(kbuf.at[slot, half, dev], kbuf.at[3, half, dev], s_fk.at[dev, half], r_k.at[3, dev, half], 2 * to + core)
+        return rcopy(kbuf.at[slot, dev, half], kbuf.at[3, dev, half], s_fwd, r_far.at[half], 2 * to + core)
 
     def body(idx, carry):
         @pl.when(idx == 1)
@@ -276,38 +266,24 @@
             for t in range(2):
                 raw_v(t).wait_recv()
                 split_v(vraw.at[t], 1 + t)
-            for half in range(2):
-                for t in range(2):
-                    got_v(1 + t, other, half)
+            arrived(r_share.at[0], 256)
             for dev in range(2):
                 fwd_v(dev, 0).start()
-            for dev in range(2):
-                got_k(2 - dev, dev, 0)
-                fwd_k(dev, 0).start()
-            got_k(1, 0, 0)
-
-        @pl.when(idx == 2)
-        def _():
-            got_k(2, 1, 0)
+            for t in range(2):
+                arrived(r_k.at[t, 0], 128)
+                fwd_k(1 - t, 0).start()
 
         @pl.when(idx == 3)
         def _():
-            for dev in range(2):
-                got_k(2 - dev, dev, 1)
-                fwd_k(dev, 1).start()
+            for t in range(2):
+                arrived(r_k.at[t, 1], 128)
+                fwd_k(1 - t, 1).start()
             for dev in range(2):
                 fwd_v(dev, 1).start()
-            got_k(1, 0, 1)
-
-        @pl.when(idx == 4)
-        def _():
-            got_k(2, 1, 1)
 
         @pl.when(idx == 5)
         def _():
-            for dev in range(2):
-                got_v(3, dev, 0)
-                got_k(3, dev, 0)
+            arrived(r_far.at[0], 256)
 
         second = (idx // 3) * (1 - idx // 5)
         slot = idx - 2 * second - 2 * (idx // 5)
@@ -328,10 +304,10 @@
             f_scr[rows, :] = val if first else f_scr[rows, :] + val
 
     def give(half, n):
-        return rcopy(ost.at[half], obuf.at[core, half], s_o.at[n], r_o.at[n], partner)
+        return rcopy(ost.at[half], obuf.at[core, half], s_o, r_o.at[n], partner)
 
     def take(half, n):
-        rcopy(ost.at[half], obuf.at[other, half], s_o.at[n], r_o.at[n], partner).wait_recv()
+        rcopy(ost.at[half], obuf.at[other, half], s_o, r_o.at[n], partner).wait_recv()
 
     for g in range(2):
         cols = pl.ds(g * HALF, HALF)
@@ -342,8 +318,7 @@
         obuf[core, done, g] = (acc[done, 1, :, cols] * (1.0 / l_scr[done, 1, :, cols])).astype(BF16)
     place(core, done, True)
 
-    for dev in range(2):
-        got_k(3, dev, 1)
+    arrived(r_far.at[1], 128)
     scores, soft, _ = tile_parts(3, last, last, False)
     s = scores(0)
     for n in range(4):
@@ -363,17 +338,16 @@
                 else:
                     lbuf[core, pl.ds(g, 1), half * HALF:(half + 1) * HALF] = val
         if dev == 0:
-            l_send = rcopy(lst, lbuf.at[core], s_l.at[0], r_l.at[0], partner)
+            l_send = rcopy(lst, lbuf.at[core], s_l, r_l.at[0], partner)
             l_send.start()
     take(done, 0)
     place(other, done, True)
 
-    for dev in range(2):
-        got_v(3, dev, 1)
+    arrived(r_far.at[2], 128)
     for n in range(4):
         cols = pl.ds((n % 2) * HALF, HALF)
         dev, g = n // 2, n % 2
-        o = nn(vbuf[3, last, 0], pbuf[n, :HALF, :]) + nn(vbuf[3, last, 1], pbuf[n, HALF:, :])
+        o = nn(vbuf[3, 0, last], pbuf[n, :HALF, :]) + nn(vbuf[3, 1, last], pbuf[n, HALF:, :])
         o = ((acc[last, dev, :, cols] + o) * (1.0 / l_scr[last, dev, :, cols])).astype(BF16)
         if dev == 0:
             ost[last, g] = o
@@ -382,7 +356,7 @@
         if n == 1:
             give(last, 1).start()
     place(core, last, False)
-    rcopy(lst, lbuf.at[other], s_l.at[0], r_l.at[0], partner).wait_recv()
+    rcopy(lst, lbuf.at[other], s_l, r_l.at[0], partner).wait_recv()
     lse = jnp.concatenate([lbuf[0, :2], lbuf[1, :2]], axis=0)
     hi = lse.astype(BF16).astype(F32)
     rest = lse - hi
@@ -390,24 +364,14 @@
     pieces = jnp.concatenate([hi, mid, rest - mid, jnp.zeros((4, ROWS), F32)], axis=0).astype(BF16)
     pieces = nn(pieces, perm[...])
     lse_out[...] = pieces[0:4] + pieces[4:8] + pieces[8:12]
+    for sem, kib in ((s_raw.at[0], 512), (s_k, 512), (s_own, 512), (s_share, 256), (s_fwd, 512)):
+        sent(sem, kib)
+    l_send.wait_send()
     take(last, 1)
     place(other, last, False)
     out_ref[...] = f_scr[...].astype(BF16)
 
-    for cp in sends:
-        cp.wait_send()
-    for t in range(2):
-        raw_v(t).wait_send()
-    for slot in range(3):
-        for half in range(2):
-            v_share(slot, half).wait_send()
-    for half in range(2):
-        for dev in range(2):
-            fwd_v(dev, half).wait_send()
-            fwd_k(dev, half).wait_send()
-    give(done, 0).wait_send()
-    give(last, 1).wait_send()
-    l_send.wait_send()
+    sent(s_o, 256)
 
 
 def write_out(o_ref, l_ref, o_hbm, l_hbm, sem):
@@ -442,8 +406,7 @@
                 vm((2, 2, 1, 2 * HALF), F32), vm((2, 2, 1, 2 * HALF), F32), vm((2, 2, D, 2 * HALF), F32),
                 vm((2, 2, D, HALF), BF16), vm((2, 2, 2, D, HALF), BF16), vm((8, ROWS), F32), vm((2, 8, ROWS), F32),
                 vm((4, 2 * HALF, HALF), BF16),
-                dma((8,)), pltpu.SemaphoreType.REGULAR, dma((2,)), dma((2,)), dma((2, 2, 2)), dma((3, 2)), dma((2,)), dma((2,)), dma((2, 2)), dma((2, 2)),
-                dma((2,)), dma((1,)), dma((4, 2, 2)), dma((4, 2, 2)), dma((2,)), dma((2,)), dma((1,)),
+                dma((8,)), pltpu.SemaphoreType.REGULAR, dma((1,)), dma((2,)), dma((1,)), dma((1,)), dma((2, 2)), dma((3,)), dma((2,)), dma((1,)),
             ],
             compiler_params=pltpu.CompilerParams(collective_id=0, has_side_effects=True, vmem_limit_bytes=40000 * 1024),
         )

time: 25.5 us -> 24.9 us (0.976)
  Pallas kernels: 24.7 us -> 24.1 us
    pallas_call x1, Pallas kernels: 23.9 us -> 23.3 us  [per_device(): out, lse = call(*args)]
where the time goes in v2:
time: 24.9 us; the launch traced here: 24.8 us
  Pallas kernels  24.1 us (97%)
  between operations  0.64 us (3%)
    pallas_call x1, Pallas kernels, per_device(): out, lse = call(*args)  23.3 us
    pallas_call x1, Pallas kernels, per_device(): pl.pallas_call(write_out, out_shape=(jax.ShapeDtypeStruct((4 * ROWS, D),...  0.81 us

profile of v2, /device:TPU:0, one launch (start us, length us, event | category | flops | bytes accessed | tf_op | source)
XLA Modules:
  0.0 24.8 jit_solution(15657131749256242121)
XLA Ops:
  0.6 23.3 %shard_map.95 = (bf16[2048,128]{1,0:T(8,128)(2,1)S(1)}, f32[4,512]{1,0:T(4,128)S(1)}) custom-call(bf16[2048,128]{1,0:T(8,128)(2,1)} %bitcast.9, bf16[1024,128]{1,0:T(8,128)(2,1)} %bitcast.10, bf16[1024,128]{1,0:T(8,128)(2,1)} %bitcast.11, s32[1,512]{1,0:T(1,128)} %bitcast.12, s32[1,512]{1,0:T(1,128)} %bitcast.13, bf16[1,128]{1,0:T(2,128)(2,1)} %bitcast.14, ...), custom_call_target="tpu_custom_call" | custom-call | tf_op jit(solution)/shard_map/pallas_call | solution.py:417
  24.0 0.8 %shard_map.96 = (bf16[2048,128]{1,0:T(8,128)(2,1)}, f32[4,512]{1,0:T(4,128)}) custom-call(bf16[2048,128]{1,0:T(8,128)(2,1)S(1)} %get-tuple-element.6.o_ref, f32[4,512]{1,0:T(4,128)S(1)} %get-tuple-element.7.l_ref), custom_call_target="tpu_custom_call" | custom-call | tf_op jit(solution)/shard_map/pallas_call | solution.py:418

commit v3 on v2

--- a/solution.py
+++ b/solution.py
@@ -29,9 +29,9 @@
     return lax.dot_general(a, b, (((1,), (0,)), ((), ())), preferred_element_type=F32)
 
 
-def kernel(q_hbm, k_hbm, v_hbm, pos_hbm, seq_hbm, qg_hbm, kg_hbm, freq_hbm, out_ref, lse_out,
-           q_in, k_in, v_in, pos_v, seq_v, qg_v, kg_v, freq_v, f_scr, cs_scr, perm, perm_t,
-           kbuf, vbuf, vraw, kst, vst, qbuf, qst, kaug, m_scr, l_scr, acc, ost, obuf, lst, lbuf, pbuf,
+def kernel(q_hbm, k_hbm, v_hbm, pos_hbm, seq_hbm, qg_hbm, kg_hbm, freq_hbm, out_ref, lse_out, lay_ref,
+           q_in, k_in, v_in, pos_v, seq_v, qg_v, kg_v, freq_v, f_scr, cs_scr, perm,
+           kbuf, vbuf, vraw, kst, vst, qbuf, qst, kaug, m_scr, l_scr, acc, ost, obuf, lst, lbuf, pbuf, abuf,
            in_sem, ready, s_raw, r_raw, r_own, r_share, r_k, r_far, r_o, r_l):
     me = lax.axis_index("cp")
     core = lax.rem(me, 2)
@@ -183,10 +183,8 @@
                 qbuf[half, dev, pl.ds(D, D), g * HALF:(g + 1) * HALF] = q_extra
     kaug[...] = jnp.concatenate([one_hot, pad], axis=0).T.astype(BF16)
 
-    dest_cols = jnp.broadcast_to(dest, (128, ROWS)).T.astype(jnp.int32)
-    for blk in range(4):
-        lanes = lax.broadcasted_iota(jnp.int32, (ROWS, 128), 1) + blk * 128
-        perm_t[blk // 2, :, (blk % 2) * 128:(blk % 2 + 1) * 128] = jnp.where(lanes == dest_cols, 1.0, 0.0).astype(BF16)
+    lane_l = lax.broadcasted_iota(jnp.int32, (8, D), 1)
+    lay_ref[...] = jnp.where(lane_l == 0, start, cnt * 0.5).astype(jnp.int32)
 
     m_scr[...] = jnp.full(m_scr.shape, NEG_BIG, F32)
     l_scr[...] = jnp.zeros(l_scr.shape, F32)
@@ -254,11 +252,43 @@
 
     def fwd_v(dev, half):
         slot, to = (2, xchip) if dev == 0 else (1, ychip)
-        return rcopy(vbuf.at[slot, dev, half], vbuf.at[3, dev, half], s_fwd, r_far.at[2 * half], 2 * to + core)
+        return rcopy(vbuf.at[slot, dev, half], vbuf.at[3, dev, half], s_fwd, r_far.at[half, 1], 2 * to + core)
 
     def fwd_k(dev, half):
         slot, to = (2, xchip) if dev == 0 else (1, ychip)
-        return rcopy(kbuf.at[slot, dev, half], kbuf.at[3, dev, half], s_fwd, r_far.at[half], 2 * to + core)
+        return rcopy(kbuf.at[slot, dev, half], kbuf.at[3, dev, half], s_fwd, r_far.at[half, 0], 2 * to + core)
+
+    done = y
+    last = 1 - y
+
+    def place(grp, half):
+        for g in range(2):
+            f_scr[pl.ds(half * 4 * HALF + 2 * grp + g, HALF, stride=4), :] = obuf[grp, half, g].astype(F32)
+
+    def pack(half):
+        rows = pl.ds(pl.multiple_of(half * 4 * HALF, 4 * HALF), 4 * HALF)
+        out_ref[rows, :] = f_scr[rows, :].astype(BF16)
+
+    def give(half, n):
+        return rcopy(ost.at[half], obuf.at[core, half], s_o, r_o.at[n], partner)
+
+    def take(half, n):
+        rcopy(ost.at[half], obuf.at[other, half], s_o, r_o.at[n], partner).wait_recv()
+
+    def early(half):
+        for g in range(2):
+            cols = pl.ds(g * HALF, HALF)
+            ost[half, g] = (acc[half, 0, :, cols] * (1.0 / l_scr[half, 0, :, cols])).T.astype(BF16)
+        give(half, 0).start()
+        for g in range(2):
+            cols = pl.ds(g * HALF, HALF)
+            obuf[core, half, g] = (acc[half, 1, :, cols] * (1.0 / l_scr[half, 1, :, cols])).T.astype(BF16)
+        place(core, half)
+
+    def take_early(half):
+        take(half, 0)
+        place(other, half)
+        pack(half)
 
     def body(idx, carry):
         @pl.when(idx == 1)
@@ -267,11 +297,11 @@
                 raw_v(t).wait_recv()
                 split_v(vraw.at[t], 1 + t)
             arrived(r_share.at[0], 256)
-            for dev in range(2):
-                fwd_v(dev, 0).start()
             for t in range(2):
                 arrived(r_k.at[t, 0], 128)
                 fwd_k(1 - t, 0).start()
+            for dev in range(2):
+                fwd_v(dev, 0).start()
 
         @pl.when(idx == 3)
         def _():
@@ -281,53 +311,49 @@
             for dev in range(2):
                 fwd_v(dev, 1).start()
 
-        @pl.when(idx == 5)
+        @pl.when((idx == 4) & (y == 0))
         def _():
-            arrived(r_far.at[0], 256)
-
-        second = (idx // 3) * (1 - idx // 5)
-        slot = idx - 2 * second - 2 * (idx // 5)
+            early(0)
+
+        second = idx // 3
+        slot = idx - 2 * second
         late_needed = (1 - y) + (idx % 2) * (y - x)
         sel = second * late_needed
         tile(slot, sel, 1 - second + sel, False)
         return carry
 
-    lax.fori_loop(0, 6, body, 0)
-
-    done = y
-    last = 1 - y
-
-    def place(grp, half, first):
-        for g in range(2):
-            rows = pl.ds(2 * grp + g, ROWS, stride=4)
-            val = nt(perm_t[half], obuf[grp, half, g])
-            f_scr[rows, :] = val if first else f_scr[rows, :] + val
-
-    def give(half, n):
-        return rcopy(ost.at[half], obuf.at[core, half], s_o, r_o.at[n], partner)
-
-    def take(half, n):
-        rcopy(ost.at[half], obuf.at[other, half], s_o, r_o.at[n], partner).wait_recv()
-
-    for g in range(2):
-        cols = pl.ds(g * HALF, HALF)
-        ost[done, g] = (acc[done, 0, :, cols] * (1.0 / l_scr[done, 0, :, cols])).astype(BF16)
-    give(done, 0).start()
-    for g in range(2):
-        cols = pl.ds(g * HALF, HALF)
-        obuf[core, done, g] = (acc[done, 1, :, cols] * (1.0 / l_scr[done, 1, :, cols])).astype(BF16)
-    place(core, done, True)
-
-    arrived(r_far.at[1], 128)
-    scores, soft, _ = tile_parts(3, last, last, False)
-    s = scores(0)
+    lax.fori_loop(0, 5, body, 0)
+
+    def weigh(khalf, qhalf):
+        scores, soft, _ = tile_parts(3, khalf, qhalf, False)
+        s = scores(0)
+        for n in range(4):
+            nxt = scores(n + 1) if n < 3 else None
+            pb, alpha = soft(n, s)
+            pbuf[n] = pb
+            abuf[n] = alpha
+            s = nxt
+
+    def weighted(n, khalf):
+        return nn(vbuf[3, 0, khalf], pbuf[n, :HALF, :]) + nn(vbuf[3, 1, khalf], pbuf[n, HALF:, :])
+
+    @pl.when(y == 0)
+    def _():
+        take_early(0)
+
+    arrived(r_far.at[0, 0], 128)
+    weigh(0, 1)
+    arrived(r_far.at[0, 1], 128)
     for n in range(4):
-        nxt = scores(n + 1) if n < 3 else None
-        pb, alpha = soft(n, s)
-        pbuf[n] = pb
         cols = pl.ds((n % 2) * HALF, HALF)
-        acc[last, n // 2, :, cols] = acc[last, n // 2, :, cols] * alpha
-        s = nxt
+        acc[1, n // 2, :, cols] = acc[1, n // 2, :, cols] * abuf[n] + weighted(n, 0)
+
+    @pl.when(y == 1)
+    def _():
+        early(1)
+
+    arrived(r_far.at[1, 0], 128)
+    weigh(last, last)
     for dev in range(2):
         for half in range(2):
             for g in range(2):
@@ -340,22 +366,22 @@
         if dev == 0:
             l_send = rcopy(lst, lbuf.at[core], s_l, r_l.at[0], partner)
             l_send.start()
-    take(done, 0)
-    place(other, done, True)
-
-    arrived(r_far.at[2], 128)
+    @pl.when(y == 1)
+    def _():
+        take_early(1)
+
+    arrived(r_far.at[1, 1], 128)
     for n in range(4):
         cols = pl.ds((n % 2) * HALF, HALF)
         dev, g = n // 2, n % 2
-        o = nn(vbuf[3, 0, last], pbuf[n, :HALF, :]) + nn(vbuf[3, 1, last], pbuf[n, HALF:, :])
-        o = ((acc[last, dev, :, cols] + o) * (1.0 / l_scr[last, dev, :, cols])).astype(BF16)
+        o = ((acc[last, dev, :, cols] * abuf[n] + weighted(n, last)) * (1.0 / l_scr[last, dev, :, cols])).T.astype(BF16)
         if dev == 0:
             ost[last, g] = o
         else:
             obuf[core, last, g] = o
         if n == 1:
             give(last, 1).start()
-    place(core, last, False)
+    place(core, last)
     rcopy(lst, lbuf.at[other], s_l, r_l.at[0], partner).wait_recv()
     lse = jnp.concatenate([lbuf[0, :2], lbuf[1, :2]], axis=0)
     hi = lse.astype(BF16).astype(F32)
@@ -368,18 +394,23 @@
         sent(sem, kib)
     l_send.wait_send()
     take(last, 1)
-    place(other, last, False)
-    out_ref[...] = f_scr[...].astype(BF16)
+    place(other, last)
+    pack(last)
 
     sent(s_o, 256)
 
 
-def write_out(o_ref, l_ref, o_hbm, l_hbm, sem):
-    copies = [pltpu.make_async_copy(o_ref, o_hbm, sem.at[0]), pltpu.make_async_copy(l_ref, l_hbm, sem.at[1])]
-    for cp in copies:
-        cp.start()
-    for cp in copies:
-        cp.wait()
+def write_out(o_ref, l_ref, lay_ref, o_hbm, l_hbm, sem):
+    lse_copy = pltpu.make_async_copy(l_ref, l_hbm, sem.at[1])
+    lse_copy.start()
+    lay = lay_ref[...]
+    for seq in range(4):
+        first, piece = lay[seq, 0], lay[seq, 1]
+        for half in range(2):
+            src = o_ref.at[pl.ds(half * HALF + first // 2, piece)]
+            pltpu.make_async_copy(src, o_hbm.at[pl.ds(first + half * piece, piece)], sem.at[0]).start()
+    pltpu.make_async_copy(o_ref, o_hbm, sem.at[0]).wait()
+    lse_copy.wait()
 
 
 def solution(mesh):
@@ -392,21 +423,21 @@
     def per_device(q_raw, k_raw, v_raw, positions, seq_ids, q_gain, k_gain):
         call = pl.pallas_call(
             kernel,
-            out_shape=(jax.ShapeDtypeStruct((4 * ROWS, D), BF16), jax.ShapeDtypeStruct((4, ROWS), F32)),
+            out_shape=(jax.ShapeDtypeStruct((4 * ROWS, D), BF16), jax.ShapeDtypeStruct((4, ROWS), F32), jax.ShapeDtypeStruct((8, D), jnp.int32)),
             in_specs=[any_spec] * 8,
-            out_specs=(pl.BlockSpec(memory_space=pltpu.VMEM), pl.BlockSpec(memory_space=pltpu.VMEM)),
+            out_specs=(pl.BlockSpec(memory_space=pltpu.VMEM),) * 3,
             scratch_shapes=[
                 vm((4 * ROWS, D), BF16), vm((2 * ROWS, D), BF16), vm((2 * ROWS, D), BF16),
                 vm((1, ROWS), jnp.int32), vm((1, ROWS), jnp.int32), vm((1, D), BF16), vm((1, D), BF16),
                 vm((64, ROWS), F32),
-                vm((4 * ROWS, D), F32), vm((2, 64, ROWS), F32), vm((ROWS, ROWS), BF16), vm((2, ROWS, HALF), BF16),
+                vm((4 * ROWS, D), F32), vm((2, 64, ROWS), F32), vm((ROWS, ROWS), BF16),
                 vm((4, 2, 2, HALF, D), BF16), vm((4, 2, 2, D, HALF), BF16),
                 vm((2, 2 * ROWS, D), BF16), vm((2, 2, HALF, D), BF16), vm((3, 2, D, HALF), BF16),
                 vm((2, 2, 2 * D, 2 * HALF), BF16), vm((2, D, 2 * HALF), BF16), vm((HALF, D), BF16),
                 vm((2, 2, 1, 2 * HALF), F32), vm((2, 2, 1, 2 * HALF), F32), vm((2, 2, D, 2 * HALF), F32),
-                vm((2, 2, D, HALF), BF16), vm((2, 2, 2, D, HALF), BF16), vm((8, ROWS), F32), vm((2, 8, ROWS), F32),
-                vm((4, 2 * HALF, HALF), BF16),
-                dma((8,)), pltpu.SemaphoreType.REGULAR, dma((1,)), dma((2,)), dma((1,)), dma((1,)), dma((2, 2)), dma((3,)), dma((2,)), dma((1,)),
+                vm((2, 2, HALF, D), BF16), vm((2, 2, 2, HALF, D), BF16), vm((8, ROWS), F32), vm((2, 8, ROWS), F32),
+                vm((4, 2 * HALF, HALF), BF16), vm((4, 1, HALF), F32),
+                dma((8,)), pltpu.SemaphoreType.REGULAR, dma((1,)), dma((2,)), dma((1,)), dma((1,)), dma((2, 2)), dma((2, 2)), dma((2,)), dma((1,)),
             ],
             compiler_params=pltpu.CompilerParams(collective_id=0, has_side_effects=True, vmem_limit_bytes=40000 * 1024),
         )
@@ -414,15 +445,15 @@
                 positions.reshape(1, ROWS), seq_ids.reshape(1, ROWS), q_gain.reshape(1, D), k_gain.reshape(1, D),
                 jnp.asarray(freq))
         args = [pltpu.with_memory_space_constraint(a, pltpu.HBM) for a in args]
-        out, lse = call(*args)
+        out, lse, lay = call(*args)
         out, lse = pl.pallas_call(
             write_out,
-            out_shape=(jax.ShapeDtypeStruct((4 * ROWS, D), BF16), jax.ShapeDtypeStruct((4, ROWS), F32)),
-            in_specs=[pl.BlockSpec(memory_space=pltpu.VMEM)] * 2,
+            out_shape=(jax.ShapeDtypeStruct((ROWS, 4, D), BF16), jax.ShapeDtypeStruct((4, ROWS), F32)),
+            in_specs=[pl.BlockSpec(memory_space=pltpu.VMEM)] * 3,
             out_specs=(pl.BlockSpec(memory_space=pltpu.HBM), pl.BlockSpec(memory_space=pltpu.HBM)),
             scratch_shapes=[dma((2,))],
-            compiler_params=pltpu.CompilerParams(vmem_limit_bytes=1024*1024),
-        )(out, lse)
-        return out.reshape(ROWS, 4, D), lse.T
+            compiler_params=pltpu.CompilerParams(vmem_limit_bytes=1024 * 1024),
+        )(out.reshape(ROWS, 4, D), lse, lay)
+        return out, lse.T
 
     return jax.shard_map(per_device, mesh=mesh, in_specs=(P("cp", "tp", None), P("cp", "tp", None), P("cp", "tp", None), P("cp"), P("cp"), P(), P()), out_specs=(P("cp", "tp", None), P("cp", "tp")), check_vma=False)

time: 24.9 us -> 24.4 us (0.980)
  Pallas kernels: 24.1 us -> 23.6 us
    pallas_call x2, Pallas kernels: 24.1 us -> 23.6 us  [the longest x1 22.7 us: per_device(): out, lse, lay = call(*args)]
where the time goes in v3:
time: 24.4 us; the launch traced here: 24.3 us
  Pallas kernels  23.6 us (97%)
  between operations  0.64 us (3%)
    pallas_call x1, Pallas kernels, per_device(): out, lse, lay = call(*args)  22.7 us
    pallas_call x1, Pallas kernels, per_device(): pl.pallas_call(write_out, out_shape=(jax.ShapeDtypeStruct((ROWS, 4, D), B...  0.89 us

profile of v3, /device:TPU:0, one launch (start us, length us, event | category | flops | bytes accessed | tf_op | source)
XLA Modules:
  0.0 24.3 jit_solution(12658655721616964324)
XLA Ops:
  0.6 22.7 %shard_map.95 = (bf16[2048,128]{1,0:T(8,128)(2,1)S(1)}, f32[4,512]{1,0:T(4,128)S(1)}, s32[8,128]{1,0:T(8,128)S(1)}) custom-call(bf16[2048,128]{1,0:T(8,128)(2,1)} %bitcast.10, bf16[1024,128]{1,0:T(8,128)(2,1)} %bitcast.11, bf16[1024,128]{1,0:T(8,128)(2,1)} %bitcast.12, s32[1,512]{1,0:T(1,128)} %bitcast.13, s32[1,512]{1,0:T(1,128)} %bitcast.14, ...), custom_call_target="tpu_custom_call" | custom-call | tf_op jit(solution)/shard_map/pallas_call | solution.py:448
  23.4 0.9 %shard_map.96 = (bf16[512,4,128]{2,1,0:T(4,128)(2,1)}, f32[4,512]{1,0:T(4,128)}) custom-call(bf16[512,4,128]{2,1,0:T(4,128)(2,1)S(1)} %bitcast.9, f32[4,512]{1,0:T(4,128)S(1)} %get-tuple-element.8.l_ref, s32[8,128]{1,0:T(8,128)S(1)} %get-tuple-element.9.lay_ref), custom_call_target="tpu_custom_call" | custom-call | tf_op jit(solution)/shard_map/pallas_call | solution.py:449

commit v4 on v3

--- a/solution.py
+++ b/solution.py
@@ -1,4 +1,3 @@
-import functools
 import math
 
 import jax
@@ -59,7 +58,7 @@
         rcopy(sized(kib), sized(kib), s_l, sem, partner).wait_recv()
 
     barrier = pltpu.get_barrier_semaphore()
-    for peer in (2 * xchip, 2 * ychip + 1, partner):
+    for peer in (2 * xchip + 1 - y, 2 * ychip + 1 - y, partner):
         pl.semaphore_signal(barrier, inc=1, device_id={"cp": peer}, device_id_type=pl.DeviceIdType.MESH)
 
     ins = [(v_hbm, v_in), (seq_hbm, seq_v), (pos_hbm, pos_v), (k_hbm, k_in), (kg_hbm, kg_v), (freq_hbm, freq_v),
@@ -75,9 +74,10 @@
         tchip = xchip + t * (ychip - xchip)
         return rcopy(v_hbm, vraw.at[t], s_raw.at[0], r_raw.at[t], 2 * tchip + core)
 
-    raw_v(core).start()
+    first = 1 - (core + y - 2 * core * y)
+    raw_v(first).start()
     pl.semaphore_wait(ready, 1)
-    raw_v(other).start()
+    raw_v(1 - first).start()
 
     in_copies[1].wait()
     seq = seq_v[...]
@@ -352,7 +352,10 @@
     def _():
         early(1)
 
-    arrived(r_far.at[1, 0], 128)
+    @pl.when(y == 0)
+    def _():
+        arrived(r_far.at[1, 0], 128)
+
     weigh(last, last)
     for dev in range(2):
         for half in range(2):
@@ -370,7 +373,10 @@
     def _():
         take_early(1)
 
-    arrived(r_far.at[1, 1], 128)
+    @pl.when(y == 0)
+    def _():
+        arrived(r_far.at[1, 1], 128)
+
     for n in range(4):
         cols = pl.ds((n % 2) * HALF, HALF)
         dev, g = n // 2, n % 2
@@ -393,6 +399,11 @@
     for sem, kib in ((s_raw.at[0], 512), (s_k, 512), (s_own, 512), (s_share, 256), (s_fwd, 512)):
         sent(sem, kib)
     l_send.wait_send()
+    @pl.when(y == 1)
+    def _():
+        for n in range(2):
+            arrived(r_far.at[1, n], 128)
+
     take(last, 1)
     place(other, last)
     pack(last)

time: 24.4 us -> 24.4 us (level)
  no operation moved by 1% of the time
where the time goes in v4:
time: 24.4 us; the launch traced here: 24.2 us
  Pallas kernels  23.6 us (97%)
  between operations  0.64 us (3%)
    pallas_call x1, Pallas kernels, per_device(): out, lse, lay = call(*args)  22.7 us
    pallas_call x1, Pallas kernels, per_device(): pl.pallas_call(write_out, out_shape=(jax.ShapeDtypeStruct((ROWS, 4, D), B...  0.91 us

profile of v4, /device:TPU:0, one launch (start us, length us, event | category | flops | bytes accessed | tf_op | source)
XLA Modules:
  0.0 24.2 jit_solution(9942563155301420559)
XLA Ops:
  0.6 22.7 %shard_map.95 = (bf16[2048,128]{1,0:T(8,128)(2,1)S(1)}, f32[4,512]{1,0:T(4,128)S(1)}, s32[8,128]{1,0:T(8,128)S(1)}) custom-call(bf16[2048,128]{1,0:T(8,128)(2,1)} %bitcast.10, bf16[1024,128]{1,0:T(8,128)(2,1)} %bitcast.11, bf16[1024,128]{1,0:T(8,128)(2,1)} %bitcast.12, s32[1,512]{1,0:T(1,128)} %bitcast.13, s32[1,512]{1,0:T(1,128)} %bitcast.14, ...), custom_call_target="tpu_custom_call" | custom-call | tf_op jit(solution)/shard_map/pallas_call | solution.py:459
  23.3 0.9 %shard_map.96 = (bf16[512,4,128]{2,1,0:T(4,128)(2,1)}, f32[4,512]{1,0:T(4,128)}) custom-call(bf16[512,4,128]{2,1,0:T(4,128)(2,1)S(1)} %bitcast.9, f32[4,512]{1,0:T(4,128)S(1)} %get-tuple-element.8.l_ref, s32[8,128]{1,0:T(8,128)S(1)} %get-tuple-element.9.lay_ref), custom_call_target="tpu_custom_call" | custom-call | tf_op jit(solution)/shard_map/pallas_call | solution.py:460

commit v5 on v4

--- a/solution.py
+++ b/solution.py
@@ -46,16 +46,16 @@
         return pltpu.make_async_remote_copy(src_ref=src, dst_ref=dst, send_sem=ssem, recv_sem=rsem,
                                             device_id={"cp": dev}, device_id_type=pl.DeviceIdType.MESH)
 
-    s_k, s_own, s_share, s_fwd, s_o, s_l = (in_sem.at[n] for n in (1, 2, 3, 4, 5, 0))
+    s_own, s_share, s_fwd, s_k, s_o = (in_sem.at[n] for n in range(5))
 
     def sized(kib):
-        return kbuf.at[pl.ds(0, kib // 256)] if kib >= 256 else kbuf.at[0, pl.ds(0, kib // 128)]
+        return f_scr.at[pl.ds(0, 2 * kib)]
 
     def sent(sem, kib):
         rcopy(sized(kib), sized(kib), sem, r_l.at[0], partner).wait_send()
 
     def arrived(sem, kib):
-        rcopy(sized(kib), sized(kib), s_l, sem, partner).wait_recv()
+        rcopy(sized(kib), sized(kib), s_o, sem, partner).wait_recv()
 
     barrier = pltpu.get_barrier_semaphore()
     for peer in (2 * xchip + 1 - y, 2 * ychip + 1 - y, partner):
@@ -63,7 +63,7 @@
 
     ins = [(v_hbm, v_in), (seq_hbm, seq_v), (pos_hbm, pos_v), (k_hbm, k_in), (kg_hbm, kg_v), (freq_hbm, freq_v),
            (q_hbm, q_in), (qg_hbm, qg_v)]
-    in_copies = [pltpu.make_async_copy(src, dst, in_sem.at[n]) for n, (src, dst) in enumerate(ins)]
+    in_copies = [pltpu.make_async_copy(src, dst, in_sem.at[n]) for n, (src, dst) in zip((2, 0, 0, 1, 3, 1, 2, 4), ins)]
     for n in (1, 2, 5, 3, 4, 0, 6, 7):
         in_copies[n].start()
 
@@ -72,14 +72,14 @@
 
     def raw_v(t):
         tchip = xchip + t * (ychip - xchip)
-        return rcopy(v_hbm, vraw.at[t], s_raw.at[0], r_raw.at[t], 2 * tchip + core)
+        return rcopy(v_hbm, vraw.at[t], s_raw.at[0], r_raw.at[0], 2 * tchip + core)
 
     first = 1 - (core + y - 2 * core * y)
     raw_v(first).start()
     pl.semaphore_wait(ready, 1)
     raw_v(1 - first).start()
 
-    in_copies[1].wait()
+    arrived(in_sem.at[0], 4)
     seq = seq_v[...]
     row_id = lax.broadcasted_iota(jnp.int32, (8, ROWS), 1).astype(F32)
     sub_id = lax.broadcasted_iota(jnp.int32, (8, ROWS), 0)
@@ -116,8 +116,7 @@
                     vst[slot, half] = part
         rcopy(vst.at[slot], vbuf.at[slot, core], s_share if slot else s_own, r_share.at[0] if slot else r_own.at[0], partner).start()
 
-    in_copies[2].wait()
-    in_copies[5].wait()
+    arrived(in_sem.at[1], 384)
     angle = freq_v[...] * pos_v[...].astype(F32)
     cs_scr[0] = jnp.cos(angle)
     cs_scr[1] = jnp.sin(angle)
@@ -132,7 +131,6 @@
         cos, sin = cs_scr[0], cs_scr[1]
         return jnp.concatenate([a * cos - b * sin, b * cos + a * sin], axis=0).astype(BF16)
 
-    in_copies[3].wait()
     in_copies[4].wait()
     f_scr[pl.ds(0, 1024), :] = k_in[...].astype(F32)
     for h in range(2):
@@ -147,10 +145,9 @@
     send_k(1)
     rcopy(kst.at[other], kbuf.at[0, core], s_own, r_own.at[0], partner).start()
 
-    in_copies[0].wait()
+    arrived(in_sem.at[2], 768)
     split_v(v_in, 0)
 
-    in_copies[6].wait()
     in_copies[7].wait()
     f_scr[...] = q_in[...].astype(F32)
 
@@ -293,8 +290,8 @@
     def body(idx, carry):
         @pl.when(idx == 1)
         def _():
+            arrived(r_raw.at[0], 512)
             for t in range(2):
-                raw_v(t).wait_recv()
                 split_v(vraw.at[t], 1 + t)
             arrived(r_share.at[0], 256)
             for t in range(2):
@@ -367,7 +364,7 @@
                 else:
                     lbuf[core, pl.ds(g, 1), half * HALF:(half + 1) * HALF] = val
         if dev == 0:
-            l_send = rcopy(lst, lbuf.at[core], s_l, r_l.at[0], partner)
+            l_send = rcopy(lst, lbuf.at[core], s_o, r_l.at[0], partner)
             l_send.start()
     @pl.when(y == 1)
     def _():
@@ -388,7 +385,7 @@
         if n == 1:
             give(last, 1).start()
     place(core, last)
-    rcopy(lst, lbuf.at[other], s_l, r_l.at[0], partner).wait_recv()
+    rcopy(lst, lbuf.at[other], s_o, r_l.at[0], partner).wait_recv()
     lse = jnp.concatenate([lbuf[0, :2], lbuf[1, :2]], axis=0)
     hi = lse.astype(BF16).astype(F32)
     rest = lse - hi
@@ -398,7 +395,6 @@
     lse_out[...] = pieces[0:4] + pieces[4:8] + pieces[8:12]
     for sem, kib in ((s_raw.at[0], 512), (s_k, 512), (s_own, 512), (s_share, 256), (s_fwd, 512)):
         sent(sem, kib)
-    l_send.wait_send()
     @pl.when(y == 1)
     def _():
         for n in range(2):
@@ -408,7 +404,7 @@
     place(other, last)
     pack(last)
 
-    sent(s_o, 256)
+    sent(s_o, 272)
 
 
 def write_out(o_ref, l_ref, lay_ref, o_hbm, l_hbm, sem):
@@ -448,7 +444,7 @@
                 vm((2, 2, 1, 2 * HALF), F32), vm((2, 2, 1, 2 * HALF), F32), vm((2, 2, D, 2 * HALF), F32),
                 vm((2, 2, HALF, D), BF16), vm((2, 2, 2, HALF, D), BF16), vm((8, ROWS), F32), vm((2, 8, ROWS), F32),
                 vm((4, 2 * HALF, HALF), BF16), vm((4, 1, HALF), F32),
-                dma((8,)), pltpu.SemaphoreType.REGULAR, dma((1,)), dma((2,)), dma((1,)), dma((1,)), dma((2, 2)), dma((2, 2)), dma((2,)), dma((1,)),
+                dma((5,)), pltpu.SemaphoreType.REGULAR, dma((1,)), dma((1,)), dma((1,)), dma((1,)), dma((2, 2)), dma((2, 2)), dma((2,)), dma((1,)),
             ],
             compiler_params=pltpu.CompilerParams(collective_id=0, has_side_effects=True, vmem_limit_bytes=40000 * 1024),
         )

time: 24.4 us -> 24.3 us (level)
  no operation moved by 1% of the time
where the time goes in v5:
time: 24.3 us; the launch traced here: 24.2 us
  Pallas kernels  23.6 us (97%)
  between operations  0.64 us (3%)
    pallas_call x1, Pallas kernels, per_device(): out, lse, lay = call(*args)  22.7 us
    pallas_call x1, Pallas kernels, per_device(): pl.pallas_call(write_out, out_shape=(jax.ShapeDtypeStruct((ROWS, 4, D), B...  0.89 us

profile of v5, /device:TPU:0, one launch (start us, length us, event | category | flops | bytes accessed | tf_op | source)
XLA Modules:
  0.0 24.2 jit_solution(3516403422023994926)
XLA Ops:
  0.6 22.7 %shard_map.95 = (bf16[2048,128]{1,0:T(8,128)(2,1)S(1)}, f32[4,512]{1,0:T(4,128)S(1)}, s32[8,128]{1,0:T(8,128)S(1)}) custom-call(bf16[2048,128]{1,0:T(8,128)(2,1)} %bitcast.10, bf16[1024,128]{1,0:T(8,128)(2,1)} %bitcast.11, bf16[1024,128]{1,0:T(8,128)(2,1)} %bitcast.12, s32[1,512]{1,0:T(1,128)} %bitcast.13, s32[1,512]{1,0:T(1,128)} %bitcast.14, ...), custom_call_target="tpu_custom_call" | custom-call | tf_op jit(solution)/shard_map/pallas_call | solution.py:455
  23.3 0.9 %shard_map.96 = (bf16[512,4,128]{2,1,0:T(4,128)(2,1)}, f32[4,512]{1,0:T(4,128)}) custom-call(bf16[512,4,128]{2,1,0:T(4,128)(2,1)S(1)} %bitcast.9, f32[4,512]{1,0:T(4,128)S(1)} %get-tuple-element.8.l_ref, s32[8,128]{1,0:T(8,128)S(1)} %get-tuple-element.9.lay_ref), custom_call_target="tpu_custom_call" | custom-call | tf_op jit(solution)/shard_map/pallas_call | solution.py:456
